TPU v7x, 512 devices: a 4x2x32 block of a 4x16x32 slice. The times are simulated.
512 devices in a mesh: survey: 2 (over y), gz: 32 (over z), gy: 4 (over x), pat: 2 (over core).
Axes of the slice: x: 4, y: 2, z: 32, core: 2. Of those that a mesh axis runs over, the one named last changes fastest.
The devices are a block of a 4x16x32 slice.
Arguments:
- conductivity: float32 [256, 512, 512], P(('survey', 'gz'), 'gy'), parts along dimension 0, may hold values from 0.3 to 3
- receivers: int32 [4, 3, 64], P(('survey', 'pat')), parts along dimension 0, may hold values from 0 to 511, as said below
- observed: float32 [4, 64], P(('survey', 'pat')), parts along dimension 0, may hold values from -6 to 6
- potential: float32 [2, 256, 512, 512], P('pat', ('survey', 'gz'), 'gy'), parts along dimension 1, may hold values from -6 to 6
- adjoint_prev: float32 [2, 256, 512, 512], P('pat', ('survey', 'gz'), 'gy'), parts along dimension 1, may hold values from -0.046875 to 0.046875
Outputs:
- adjoint: float32 [2, 256, 512, 512], P('pat', ('survey', 'gz'), 'gy'), parts along dimension 1
- gradient: float32 [256, 512, 512], P(('survey', 'gz'), 'gy'), parts along dimension 0
There are 2 independent parts, one for each index of `survey`. A program takes and returns all parts, laid end to end along the dimension named above; each array names one. Nothing has to cross between parts.
Inputs may be any that keep to these rules, and one draw needn't show every extreme that they name: receivers[p, 0, r], receivers[p, 1, r] and receivers[p, 2, r] are a z cell below 128, a y cell below 512 and an x cell below 512; several receivers may share a cell.
All inputs are finite; a program needn't handle non-finite values.
Results may differ from a plain program's by a relative error of at most 0.0003.
Values sent between devices are 32-bit elements; how exact they have to be, the bound alone decides.
No kernel may reach another device: no remote copies, remote signals or barrier semaphores. Data moves between devices by JAX's collectives and lax.ppermute only.
A program may use at most 64 MiB of HBM per device.

v0:
```python
import jax
import jax.numpy as jnp
from jax import lax
from jax.sharding import PartitionSpec as P

relax_weight = 0.8


def extended_2(x, sides, width):
    edges = {}
    for axis, dim in sides:
        devices, length = (lax.axis_size(axis), x.shape[dim])
        up = [(i, (i + 1) % devices) for i in range(devices - 1)]
        last = lax.slice_in_dim(x, length - width, length, axis=dim)
        first = lax.slice_in_dim(x, 0, width, axis=dim)
        edges[dim] = (
            lax.ppermute(last, axis, up),
            lax.ppermute(first, axis, [(b, a) for a, b in up]),
        )
    done = []
    for _, dim in sides:
        low, high = edges[dim]
        around = [(width, width) if d in done else (0, 0) for d in range(x.ndim)]
        x = jnp.concatenate([jnp.pad(low, around), x, jnp.pad(high, around)], axis=dim)
        done.append(dim)
    return x


def from_everyone(x, axis):
    devices = lax.axis_size(axis)
    return lax.all_to_all(jnp.broadcast_to(x[None], (devices, *x.shape)), axis, 0, 0, tiled=True)


def taken_together(x, axis):
    return from_everyone(x, axis).sum(axis=0)


def beside_cells(extended):
    widened = jnp.pad(extended, [(0, 0)] * (extended.ndim - 1) + [(1, 1)])
    centre = widened[..., 1:-1, 1:-1, 1:-1]
    others = [
        widened[..., 2:, 1:-1, 1:-1],
        widened[..., :-2, 1:-1, 1:-1],
        widened[..., 1:-1, 2:, 1:-1],
        widened[..., 1:-1, :-2, 1:-1],
        widened[..., 1:-1, 1:-1, 2:],
        widened[..., 1:-1, 1:-1, :-2],
    ]
    return (centre, others)


def relax(cond_ext, adjoint_ext, source):
    cond_mid, cond_near = beside_cells(cond_ext)
    adj_mid, adj_near = beside_cells(adjoint_ext)
    diagonal = jnp.zeros_like(cond_mid)
    coupled = jnp.zeros_like(adj_mid)
    for cond_side, adj_side in zip(cond_near, adj_near):
        face_coef = 0.5 * (cond_mid + cond_side)
        diagonal = diagonal + face_coef
        coupled = coupled + face_coef * adj_side
    updated = adj_mid + relax_weight * (source - diagonal * adj_mid + coupled) / diagonal
    return updated


def contribution(pot_ext, adj_ext):
    pot_mid, pot_near = beside_cells(pot_ext)
    adj_mid, adj_near = beside_cells(adj_ext)
    summed = jnp.zeros_like(adj_mid)
    for pot_side, adj_side in zip(pot_near, adj_near):
        summed = summed + (pot_mid - pot_side) * (adj_mid - adj_side)
    return -0.5 * jnp.sum(summed, axis=0)


def receiver_source(field, receivers, observed, z_start, y_start):
    z_count = field.shape[1]
    y_count = field.shape[2]
    z_local = receivers[:, 0, :] - z_start
    y_local = receivers[:, 1, :] - y_start
    x_local = receivers[:, 2, :]
    inside = (z_local >= 0) & (z_local < z_count) & (y_local >= 0) & (y_local < y_count)
    z_local = jnp.clip(z_local, 0, z_count - 1)
    y_local = jnp.clip(y_local, 0, y_count - 1)
    pattern_ids = jnp.broadcast_to(
        jnp.arange(field.shape[0], dtype=jnp.int32)[:, None], z_local.shape
    )
    values = jnp.where(
        inside, field[pattern_ids, z_local, y_local, x_local] - observed, jnp.zeros_like(observed)
    )
    return jnp.zeros_like(field).at[pattern_ids, z_local, y_local, x_local].add(values)


def local(conductivity, receivers, observed, potential, adjoint_prev):
    pattern_count = potential.shape[0]
    z_cells = conductivity.shape[0]
    y_cells = conductivity.shape[1]
    z_first = lax.axis_index("gz") * z_cells
    y_first = lax.axis_index("gy") * y_cells
    stacked = jnp.concatenate([conductivity[None], adjoint_prev], axis=0)
    extended = extended_2(stacked, (("gz", 1), ("gy", 2)), 1)
    cond_ext = extended[0]
    source = receiver_source(potential, receivers, observed, z_first, y_first)
    adjoint = relax(cond_ext, extended[1:], source)
    rimmed = extended_2(adjoint, (("gz", 1), ("gy", 2)), 1)
    adjoint = relax(cond_ext, rimmed, source)
    both_ext = extended_2(jnp.concatenate([potential, adjoint], axis=0), (("gz", 1), ("gy", 2)), 1)
    partial_grad = contribution(both_ext[:pattern_count], both_ext[pattern_count:])
    gradient = taken_together(partial_grad, "pat")
    return (adjoint, gradient)


def solution(mesh):
    return jax.shard_map(
        local,
        mesh=mesh,
        in_specs=(
            P(("survey", "gz"), "gy", None),
            P(("survey", "pat"), None, None),
            P(("survey", "pat"), None),
            P("pat", ("survey", "gz"), "gy", None),
            P("pat", ("survey", "gz"), "gy", None),
        ),
        out_specs=(P("pat", ("survey", "gz"), "gy", None), P(("survey", "gz"), "gy", None)),
        check_vma=False,
    )
```

profile of v0, /device:TPU:33, one launch (start us, length us, event | category | flops | bytes accessed | tf_op | source)
XLA Modules:
  0.0 116.9 jit_solution(10397924429199837452)
XLA Ops:
  0.6 1.1 pad_maximum_fusion.38
  1.8 4.2 %collective-permute-start = (f32[2,4,1,512]{3,2,1,0:T(1,128)S(1)}, f32[2,4,1,512]{3,2,1,0:T(1,128)S(1)}, u32[]{:S(2)}, u32[]{:S(2)}) collective-permute-start(f32[2,4,1,512]{3,2,1,0:T(1,128)S(1)} %get-tuple-element.10), channel_id=1, source_target_pairs={{0,2},{2,4},{4,6},{1,3},{3,5},{5,7},{8,10},{10,12},{12,14},{9,11},... | collective-permute-start | bytes 49160 | tf_op jit(solution)/shard_map/ppermute | solution.py:17
  6.0 1.3 %collective-permute-start.3 = (f32[2,4,1,512]{3,2,1,0:T(1,128)S(1)}, f32[2,4,1,512]{3,2,1,0:T(1,128)S(1)}, u32[]{:S(2)}, u32[]{:S(2)}) collective-permute-start(f32[2,4,1,512]{3,2,1,0:T(1,128)S(1)} %get-tuple-element.11), channel_id=1, source_target_pairs={{2,0},{4,2},{6,4},{3,1},{5,3},{7,5},{10,8},{12,10},{14,12},{11,9},... | collective-permute-start | bytes 49160 | tf_op jit(solution)/shard_map/ppermute | solution.py:18
  7.4 1.0 pad_maximum_fusion.35
  8.4 5.2 %collective-permute-start.1 = (f32[2,1,128,512]{3,2,1,0:T(8,128)}, f32[2,1,128,512]{3,2,1,0:T(8,128)}, u32[]{:S(2)}, u32[]{:S(2)}) collective-permute-start(f32[2,1,128,512]{3,2,1,0:T(8,128)} %get-tuple-element.12), channel_id=1, source_target_pairs={{0,8},{8,16},{16,24},{24,32},{32,40},{40,48},{48,56},{56,64},{64,7... | collective-permute-start | bytes 1572872 | tf_op jit(solution)/shard_map/ppermute | solution.py:17
  13.6 1.3 %collective-permute-start.2 = (f32[2,1,128,512]{3,2,1,0:T(8,128)}, f32[2,1,128,512]{3,2,1,0:T(8,128)}, u32[]{:S(2)}, u32[]{:S(2)}) collective-permute-start(f32[2,1,128,512]{3,2,1,0:T(8,128)} %get-tuple-element.13), channel_id=1, source_target_pairs={{8,0},{16,8},{24,16},{32,24},{40,32},{48,40},{56,48},{64,56},{72,6... | collective-permute-start | bytes 1572872 | tf_op jit(solution)/shard_map/ppermute | solution.py:18
  15.0 1.0 gather_fusion
  16.1 1.1 broadcast.284
  17.2 9.7 %scatter_fusion = f32[4,128,512]{2,1,0:T(8,128)} fusion(f32[4,128,512]{2,1,0:T(8,128)} %broadcast.284, s32[64]{0:T(128)S(1)} %get-tuple-element.19, f32[64]{0:T(128)S(1)} %fusion.66), kind=kCustom, calls=%fused_computation.1 | custom fusion | flops 64 | bytes 1536 | tf_op jit(solution)/shard_map/scatter-add | solution.py:89
  26.9 1.7 %pad_maximum_fusion = f32[2,6,130,512]{3,2,1,0:T(8,128)S(1)} fusion(f32[2,6,1,512]{3,2,1,0:T(1,128)S(1)} %pad.39, f32[2,1,128,512]{3,2,1,0:T(8,128)} %collective-permute-done.2, f32[1,4,128,512]{3,2,1,0:T(8,128)S(1)} %copy-done.2, f32[1,4,128,512]{3,2,1,0:T(8,128)S(1)} %bitcast.65, f32[2,1,128,512]{3,2,1,0:T(8,128)} %collective-permute-done.1, ...), kind=kLoop, calls=%fused_computation.2 | loop fusion | flops 3993600 | bytes 6389760 | tf_op jit(solution)/shard_map/concatenate | solution.py:24
  28.6 0.4 slice_bitcast_fusion
  29.0 0.9 copy-done.4
  29.8 4.7 %fusion.11 = f32[1,4,128,512]{3,2,1,0:T(8,128)S(1)} fusion(f32[1,4,128,512]{3,2,1,0:T(8,128)S(1)} %copy-done.2, f32[1,6,130,512]{3,2,1,0:T(8,128)S(1)} %get-tuple-element.5, f32[2,6,1,512]{3,2,1,0:T(1,128)S(1)} %pad.38, f32[2,1,128,512]{3,2,1,0:T(8,128)} %collective-permute-done.2, f32[2,1,128,512]{3,2,1,0:T(8,128)} %collective-permute-done.1, ...), kind=kLoop, calls=%fused_computation.36 | loop fusion | flops 12058624 | bytes 13877248 | tf_op jit(solution)/shard_map/add | solution.py:61
  34.5 6.2 %collective-permute-start.5 = (f32[1,1,128,512]{3,2,1,0:T(8,128)S(1)}, f32[1,1,128,512]{3,2,1,0:T(8,128)S(1)}, u32[]{:S(2)}, u32[]{:S(2)}) collective-permute-start(f32[1,1,128,512]{3,2,1,0:T(8,128)S(1)} %get-tuple-element.14), channel_id=1, source_target_pairs={{0,8},{8,16},{16,24},{24,32},{32,40},{40,48},{48,56},{56,64},{64,7... | collective-permute-start | bytes 786440 | tf_op jit(solution)/shard_map/ppermute | solution.py:17
  40.8 1.3 %collective-permute-start.4 = (f32[1,1,128,512]{3,2,1,0:T(8,128)S(1)}, f32[1,1,128,512]{3,2,1,0:T(8,128)S(1)}, u32[]{:S(2)}, u32[]{:S(2)}) collective-permute-start(f32[1,1,128,512]{3,2,1,0:T(8,128)S(1)} %get-tuple-element.15), channel_id=1, source_target_pairs={{8,0},{16,8},{24,16},{32,24},{40,32},{48,40},{56,48},{64,56},{72,6... | collective-permute-start | bytes 786440 | tf_op jit(solution)/shard_map/ppermute | solution.py:18
  42.1 3.8 %collective-permute-start.7 = (f32[1,4,1,512]{3,2,1,0:T(1,128)S(1)}, f32[1,4,1,512]{3,2,1,0:T(1,128)S(1)}, u32[]{:S(2)}, u32[]{:S(2)}) collective-permute-start(f32[1,4,1,512]{3,2,1,0:T(1,128)S(1)} %get-tuple-element.16), channel_id=1, source_target_pairs={{0,2},{2,4},{4,6},{1,3},{3,5},{5,7},{8,10},{10,12},{12,14},{9,11},... | collective-permute-start | bytes 24584 | tf_op jit(solution)/shard_map/ppermute | solution.py:17
  45.9 1.3 %collective-permute-start.6 = (f32[1,4,1,512]{3,2,1,0:T(1,128)S(1)}, f32[1,4,1,512]{3,2,1,0:T(1,128)S(1)}, u32[]{:S(2)}, u32[]{:S(2)}) collective-permute-start(f32[1,4,1,512]{3,2,1,0:T(1,128)S(1)} %get-tuple-element.17), channel_id=1, source_target_pairs={{2,0},{4,2},{6,4},{3,1},{5,3},{7,5},{10,8},{12,10},{14,12},{11,9},... | collective-permute-start | bytes 24584 | tf_op jit(solution)/shard_map/ppermute | solution.py:18
  47.2 3.1 %collective-permute-done.6 = f32[1,4,1,512]{3,2,1,0:T(1,128)S(1)} collective-permute-done((f32[1,4,1,512]{3,2,1,0:T(1,128)S(1)}, f32[1,4,1,512]{3,2,1,0:T(1,128)S(1)}, u32[]{:S(2)}, u32[]{:S(2)}) %collective-permute-start.6) | collective-permute-done | bytes 8224 | tf_op jit(solution)/shard_map/ppermute | solution.py:18
  50.3 0.7 select_maximum_fusion
  51.1 3.4 %fusion.38 = f32[1,4,128,512]{3,2,1,0:T(8,128)S(1)} fusion(f32[1,4,128,512]{3,2,1,0:T(8,128)S(1)} %fusion.11, f32[1,6,130,514]{3,2,1,0:T(8,128)S(1)} %select_maximum_fusion, f32[1,6,1,512]{3,2,1,0:T(1,128)S(1)} %pad.43, f32[1,1,128,512]{3,2,1,0:T(8,128)S(1)} %collective-permute-done.4, f32[1,1,128,512]{3,2,1,0:T(8,128)S(1)} %collective-permute-done.5, ...), kind=kLoop, calls=%fused_computation.80 | loop fusion | flops 11010048 | bytes 12705792 | tf_op jit(solution)/shard_map/add | solution.py:61
  54.6 6.7 %collective-permute-start.9 = (f32[2,1,128,512]{3,2,1,0:T(8,128)S(1)}, f32[2,1,128,512]{3,2,1,0:T(8,128)S(1)}, u32[]{:S(2)}, u32[]{:S(2)}) collective-permute-start(f32[2,1,128,512]{3,2,1,0:T(8,128)S(1)} %get-tuple-element.8), channel_id=1, source_target_pairs={{0,8},{8,16},{16,24},{24,32},{32,40},{40,48},{48,56},{56,64},{64,7... | collective-permute-start | bytes 1572872 | tf_op jit(solution)/shard_map/ppermute | solution.py:17
  61.3 1.3 %collective-permute-start.8 = (f32[2,1,128,512]{3,2,1,0:T(8,128)S(1)}, f32[2,1,128,512]{3,2,1,0:T(8,128)S(1)}, u32[]{:S(2)}, u32[]{:S(2)}) collective-permute-start(f32[2,1,128,512]{3,2,1,0:T(8,128)S(1)} %get-tuple-element.9), channel_id=1, source_target_pairs={{8,0},{16,8},{24,16},{32,24},{40,32},{48,40},{56,48},{64,56},{72,6... | collective-permute-start | bytes 1572872 | tf_op jit(solution)/shard_map/ppermute | solution.py:18
  62.7 3.3 %collective-permute-start.11 = (f32[2,4,1,512]{3,2,1,0:T(1,128)S(1)}, f32[2,4,1,512]{3,2,1,0:T(1,128)S(1)}, u32[]{:S(2)}, u32[]{:S(2)}) collective-permute-start(f32[2,4,1,512]{3,2,1,0:T(1,128)S(1)} %get-tuple-element.6), channel_id=1, source_target_pairs={{0,2},{2,4},{4,6},{1,3},{3,5},{5,7},{8,10},{10,12},{12,14},{9,11},... | collective-permute-start | bytes 49160 | tf_op jit(solution)/shard_map/ppermute | solution.py:17
  66.0 1.3 %collective-permute-start.10 = (f32[2,4,1,512]{3,2,1,0:T(1,128)S(1)}, f32[2,4,1,512]{3,2,1,0:T(1,128)S(1)}, u32[]{:S(2)}, u32[]{:S(2)}) collective-permute-start(f32[2,4,1,512]{3,2,1,0:T(1,128)S(1)} %get-tuple-element.7), channel_id=1, source_target_pairs={{2,0},{4,2},{6,4},{3,1},{5,3},{7,5},{10,8},{12,10},{14,12},{11,9},... | collective-permute-start | bytes 49160 | tf_op jit(solution)/shard_map/ppermute | solution.py:18
  67.3 3.2 %collective-permute-done.10 = f32[2,4,1,512]{3,2,1,0:T(1,128)S(1)} collective-permute-done((f32[2,4,1,512]{3,2,1,0:T(1,128)S(1)}, f32[2,4,1,512]{3,2,1,0:T(1,128)S(1)}, u32[]{:S(2)}, u32[]{:S(2)}) %collective-permute-start.10) | collective-permute-done | bytes 16416 | tf_op jit(solution)/shard_map/ppermute | solution.py:18
  70.5 1.6 %collective-permute-done.8 = f32[2,1,128,512]{3,2,1,0:T(8,128)S(1)} collective-permute-done((f32[2,1,128,512]{3,2,1,0:T(8,128)S(1)}, f32[2,1,128,512]{3,2,1,0:T(8,128)S(1)}, u32[]{:S(2)}, u32[]{:S(2)}) %collective-permute-start.8) | collective-permute-done | bytes 524320 | tf_op jit(solution)/shard_map/ppermute | solution.py:18
  72.1 0.4 pad_maximum_fusion.1
  72.5 0.3 fusion.67
  72.9 3.5 %fusion.18 = f32[4,128,512]{2,1,0:T(8,128)S(1)} fusion(f32[1,4,128,512]{3,2,1,0:T(8,128)S(1)} %copy-done.1, f32[1,6,130,512]{3,2,1,0:T(8,128)S(1)} %get-tuple-element.3, f32[1,4,128,512]{3,2,1,0:T(8,128)S(1)} %fusion.38, f32[1,6,130,512]{3,2,1,0:T(8,128)S(1)} %get-tuple-element.2, f32[2,6,1,512]{3,2,1,0:T(1,128)S(1)} %pad.46, ...), kind=kLoop, calls=%fused_computation.43 | loop fusion | flops 12582912 | bytes 7438336 | tf_op jit(solution)/shard_map/broadcast_in_dim | solution.py:31
  76.4 0.2 broadcast_in_dim.64
  76.6 39.0 %all_to_all.5 = f32[2,4,128,512]{3,2,1,0:T(8,128)S(1)} all-to-all(f32[2,4,128,512]{3,2,1,0:T(8,128)S(1)} %broadcast_in_dim.64), channel_id=1, replica_groups=mesh['survey'=2,'gz'=32,'gy'=4,'pat'=2] {'pat'}, dimensions={0} | all-to-all | bytes 4194304 | tf_op jit(solution)/shard_map/all_to_all | solution.py:31
  115.7 1.2 %reduce_sum.8 = f32[4,128,512]{2,1,0:T(8,128)} reduce(f32[2,4,128,512]{3,2,1,0:T(8,128)S(1)} %all_to_all.5, f32[]{:T(128)} %constant.13.clone.1), dimensions={0}, to_apply=%region_1.2 | reduce | flops 262144 | bytes 3145732 | tf_op jit(solution)/shard_map/reduce_sum | solution.py:35
  (37 shorter events, 0.3 us)
Async XLA Ops:
  0.6 6.7 %copy-start.2 = (f32[1,4,128,512]{3,2,1,0:T(8,128)S(1)}, f32[1,4,128,512]{3,2,1,0:T(8,128)}, u32[]{:S(2)}) copy-start(f32[1,4,128,512]{3,2,1,0:T(8,128)} %param.9) | copy-start | bytes 3145732
  0.6 6.7 %copy-start.3 = (f32[4,128,512]{2,1,0:T(8,128)S(1)}, f32[4,128,512]{2,1,0:T(8,128)}, u32[]{:S(2)}) copy-start(f32[4,128,512]{2,1,0:T(8,128)} %param.5) | copy-start | bytes 3145732
  1.8 13.2 %copy-start.5 = (s32[1,3,64]{2,0,1:T(1,128)S(1)}, s32[1,3,64]{2,0,1:T(1,128)}, u32[]{:S(2)}) copy-start(s32[1,3,64]{2,0,1:T(1,128)} %param.6) | copy-start | bytes 2308
  1.8 13.3 %copy-start.1 = (f32[1,4,128,512]{3,2,1,0:T(8,128)S(1)}, f32[1,4,128,512]{3,2,1,0:T(8,128)}, u32[]{:S(2)}) copy-start(f32[1,4,128,512]{3,2,1,0:T(8,128)} %param.8) | copy-start | bytes 3145732
  1.8 14.3 %copy-start.6 = (f32[1,64]{1,0:T(1,128)S(1)}, f32[1,64]{1,0:T(1,128)}, u32[]{:S(2)}) copy-start(f32[1,64]{1,0:T(1,128)} %param.7) | copy-start | bytes 772
  1.8 25.1 %collective-permute-start = (f32[2,4,1,512]{3,2,1,0:T(1,128)S(1)}, f32[2,4,1,512]{3,2,1,0:T(1,128)S(1)}, u32[]{:S(2)}, u32[]{:S(2)}) collective-permute-start(f32[2,4,1,512]{3,2,1,0:T(1,128)S(1)} %get-tuple-element.10), channel_id=1, source_target_pairs={{0,2},{2,4},{4,6},{1,3},{3,5},{5,7},{8,10},{10,12},{12,14},{9,11},... | collective-permute-start | bytes 49160 | tf_op jit(solution)/shard_map/ppermute | solution.py:17
  6.0 20.8 %collective-permute-start.3 = (f32[2,4,1,512]{3,2,1,0:T(1,128)S(1)}, f32[2,4,1,512]{3,2,1,0:T(1,128)S(1)}, u32[]{:S(2)}, u32[]{:S(2)}) collective-permute-start(f32[2,4,1,512]{3,2,1,0:T(1,128)S(1)} %get-tuple-element.11), channel_id=1, source_target_pairs={{2,0},{4,2},{6,4},{3,1},{5,3},{7,5},{10,8},{12,10},{14,12},{11,9},... | collective-permute-start | bytes 49160 | tf_op jit(solution)/shard_map/ppermute | solution.py:18
  8.4 18.5 %collective-permute-start.1 = (f32[2,1,128,512]{3,2,1,0:T(8,128)}, f32[2,1,128,512]{3,2,1,0:T(8,128)}, u32[]{:S(2)}, u32[]{:S(2)}) collective-permute-start(f32[2,1,128,512]{3,2,1,0:T(8,128)} %get-tuple-element.12), channel_id=1, source_target_pairs={{0,8},{8,16},{16,24},{24,32},{32,40},{40,48},{48,56},{56,64},{64,7... | collective-permute-start | bytes 1572872 | tf_op jit(solution)/shard_map/ppermute | solution.py:17
  13.6 13.3 %collective-permute-start.2 = (f32[2,1,128,512]{3,2,1,0:T(8,128)}, f32[2,1,128,512]{3,2,1,0:T(8,128)}, u32[]{:S(2)}, u32[]{:S(2)}) collective-permute-start(f32[2,1,128,512]{3,2,1,0:T(8,128)} %get-tuple-element.13), channel_id=1, source_target_pairs={{8,0},{16,8},{24,16},{32,24},{40,32},{48,40},{56,48},{64,56},{72,6... | collective-permute-start | bytes 1572872 | tf_op jit(solution)/shard_map/ppermute | solution.py:18
  28.6 1.2 %copy-start.4 = (f32[4,128,512]{2,1,0:T(8,128)S(1)}, f32[4,128,512]{2,1,0:T(8,128)}, u32[]{:S(2)}) copy-start(f32[4,128,512]{2,1,0:T(8,128)} %scatter_fusion) | copy-start | bytes 3145732
  34.5 15.8 %collective-permute-start.5 = (f32[1,1,128,512]{3,2,1,0:T(8,128)S(1)}, f32[1,1,128,512]{3,2,1,0:T(8,128)S(1)}, u32[]{:S(2)}, u32[]{:S(2)}) collective-permute-start(f32[1,1,128,512]{3,2,1,0:T(8,128)S(1)} %get-tuple-element.14), channel_id=1, source_target_pairs={{0,8},{8,16},{16,24},{24,32},{32,40},{40,48},{48,56},{56,64},{64,7... | collective-permute-start | bytes 786440 | tf_op jit(solution)/shard_map/ppermute | solution.py:17
  40.8 9.6 %collective-permute-start.4 = (f32[1,1,128,512]{3,2,1,0:T(8,128)S(1)}, f32[1,1,128,512]{3,2,1,0:T(8,128)S(1)}, u32[]{:S(2)}, u32[]{:S(2)}) collective-permute-start(f32[1,1,128,512]{3,2,1,0:T(8,128)S(1)} %get-tuple-element.15), channel_id=1, source_target_pairs={{8,0},{16,8},{24,16},{32,24},{40,32},{48,40},{56,48},{64,56},{72,6... | collective-permute-start | bytes 786440 | tf_op jit(solution)/shard_map/ppermute | solution.py:18
  42.1 5.1 %collective-permute-start.7 = (f32[1,4,1,512]{3,2,1,0:T(1,128)S(1)}, f32[1,4,1,512]{3,2,1,0:T(1,128)S(1)}, u32[]{:S(2)}, u32[]{:S(2)}) collective-permute-start(f32[1,4,1,512]{3,2,1,0:T(1,128)S(1)} %get-tuple-element.16), channel_id=1, source_target_pairs={{0,2},{2,4},{4,6},{1,3},{3,5},{5,7},{8,10},{10,12},{12,14},{9,11},... | collective-permute-start | bytes 24584 | tf_op jit(solution)/shard_map/ppermute | solution.py:17
  45.9 4.4 %collective-permute-start.6 = (f32[1,4,1,512]{3,2,1,0:T(1,128)S(1)}, f32[1,4,1,512]{3,2,1,0:T(1,128)S(1)}, u32[]{:S(2)}, u32[]{:S(2)}) collective-permute-start(f32[1,4,1,512]{3,2,1,0:T(1,128)S(1)} %get-tuple-element.17), channel_id=1, source_target_pairs={{2,0},{4,2},{6,4},{3,1},{5,3},{7,5},{10,8},{12,10},{14,12},{11,9},... | collective-permute-start | bytes 24584 | tf_op jit(solution)/shard_map/ppermute | solution.py:18
  54.5 18.4 %copy-start = (f32[1,4,128,512]{3,2,1,0:T(8,128)}, f32[1,4,128,512]{3,2,1,0:T(8,128)S(1)}, u32[]{:S(2)}) copy-start(f32[1,4,128,512]{3,2,1,0:T(8,128)S(1)} %fusion.38) | copy-start | bytes 3145732
  54.6 15.9 %collective-permute-start.9 = (f32[2,1,128,512]{3,2,1,0:T(8,128)S(1)}, f32[2,1,128,512]{3,2,1,0:T(8,128)S(1)}, u32[]{:S(2)}, u32[]{:S(2)}) collective-permute-start(f32[2,1,128,512]{3,2,1,0:T(8,128)S(1)} %get-tuple-element.8), channel_id=1, source_target_pairs={{0,8},{8,16},{16,24},{24,32},{32,40},{40,48},{48,56},{56,64},{64,7... | collective-permute-start | bytes 1572872 | tf_op jit(solution)/shard_map/ppermute | solution.py:17
  61.3 10.8 %collective-permute-start.8 = (f32[2,1,128,512]{3,2,1,0:T(8,128)S(1)}, f32[2,1,128,512]{3,2,1,0:T(8,128)S(1)}, u32[]{:S(2)}, u32[]{:S(2)}) collective-permute-start(f32[2,1,128,512]{3,2,1,0:T(8,128)S(1)} %get-tuple-element.9), channel_id=1, source_target_pairs={{8,0},{16,8},{24,16},{32,24},{40,32},{48,40},{56,48},{64,56},{72,6... | collective-permute-start | bytes 1572872 | tf_op jit(solution)/shard_map/ppermute | solution.py:18
  62.7 4.6 %collective-permute-start.11 = (f32[2,4,1,512]{3,2,1,0:T(1,128)S(1)}, f32[2,4,1,512]{3,2,1,0:T(1,128)S(1)}, u32[]{:S(2)}, u32[]{:S(2)}) collective-permute-start(f32[2,4,1,512]{3,2,1,0:T(1,128)S(1)} %get-tuple-element.6), channel_id=1, source_target_pairs={{0,2},{2,4},{4,6},{1,3},{3,5},{5,7},{8,10},{10,12},{12,14},{9,11},... | collective-permute-start | bytes 49160 | tf_op jit(solution)/shard_map/ppermute | solution.py:17
  66.0 4.5 %collective-permute-start.10 = (f32[2,4,1,512]{3,2,1,0:T(1,128)S(1)}, f32[2,4,1,512]{3,2,1,0:T(1,128)S(1)}, u32[]{:S(2)}, u32[]{:S(2)}) collective-permute-start(f32[2,4,1,512]{3,2,1,0:T(1,128)S(1)} %get-tuple-element.7), channel_id=1, source_target_pairs={{2,0},{4,2},{6,4},{3,1},{5,3},{7,5},{10,8},{12,10},{14,12},{11,9},... | collective-permute-start | bytes 49160 | tf_op jit(solution)/shard_map/ppermute | solution.py:18
where the time goes:
time: 118 us; the launch traced here: 117 us
  blocking collectives  39 us (33%)
  starting transfers between devices  37.3 us (32%)
  other arithmetic  27.6 us (23%)
  waiting for transfers between devices  7.83 us (7%)
  local copies, waits for them, and re-layouts  4.08 us (3%)
    all_to_all x1, blocking collectives, from_everyone(): lax.all_to_all(jnp.broadcast_to(x[None], (devices, *x.shape)), axis, 0, 0...  39 us
    ppermute x6, starting transfers between devices, extended_2(): lax.ppermute(last, axis, up)  29.4 us
    scatter-add x1, other arithmetic, receiver_source(): jnp.zeros_like(field).at[pattern_ids, z_local, y_local, x_local].add(values)  9.7 us
    add x2, other arithmetic, relax(): adj_mid + relax_weight * (source - diagonal * adj_mid + coupled) / diagonal  8.08 us
    ppermute x6, starting transfers between devices, extended_2(): lax.ppermute(first, axis, [(b, a) for a, b in up])  7.84 us
    ppermute x6, waiting for transfers between devices, extended_2(): lax.ppermute(first, axis, [(b, a) for a, b in up])  7.81 us
    broadcast_in_dim x1, other arithmetic, from_everyone(): jnp.broadcast_to(x[None], (devices, *x.shape))  3.47 us
    concatenate x3, other arithmetic, extended_2(): jnp.concatenate([jnp.pad(low, around), x, jnp.pad(high, around)], axis=dim)  2.84 us
  transfers between devices with their start and end apart: 12, of which 3 were waited for; matrix products, arithmetic and copies ran while one was open for 11% of the time, Pallas kernels for 0%

commit v1 on v0

v1 whole, which is shorter than its diff:
```python
import jax
import jax.numpy as jnp
from jax import lax
from jax.experimental import pallas as pl
from jax.experimental.pallas import tpu as pltpu
from jax.sharding import PartitionSpec as P


F32 = jnp.float32
VMEM = pl.BlockSpec(memory_space=pltpu.VMEM)
SMEM = pl.BlockSpec(memory_space=pltpu.SMEM)
HBM = pl.BlockSpec(memory_space=pltpu.HBM)
W = 3


def pack_kernel(
    rec_hbm, obs_hbm, cond, adj, pot,
    z_down, z_up, c_down, c_up, y_down, y_up, down_down, down_up, up_down, up_up,
    picked, field, rims, rec, obs, near, edge_sem, field_sem, plane_sem, list_sem,
):
    z_cells, y_cells, lanes = pot.shape
    count = obs.shape[1]
    lists = [
        pltpu.make_async_copy(rec_hbm, rec, list_sem.at[0]),
        pltpu.make_async_copy(obs_hbm, obs, list_sem.at[1]),
    ]
    for copy in lists:
        copy.start()
    z_first = lax.axis_index("gz") * z_cells
    y_first = lax.axis_index("gy") * y_cells
    end = y_cells - 8
    last = (W + 1) * y_cells
    edges = [
        pltpu.make_async_copy(x.at[:, pl.ds(first, 8), :], rims.at[i], edge_sem.at[i])
        for i, (x, first) in enumerate((x, first) for x in (cond, adj, pot) for first in (0, end))
    ]
    fields = [
        pltpu.make_async_copy(pot.at[k], field.at[k], field_sem.at[k]) for k in range(z_cells)
    ]
    moves = []
    for k in range(W):
        rows = pl.ds(k * y_cells, y_cells)
        top = z_cells - W + k
        moves += [(adj.at[top], z_up.at[rows]), (adj.at[k], z_down.at[rows])]
        moves += [(cond.at[top], c_up.at[k]), (cond.at[k], c_down.at[k])]
    rows = pl.ds(W * y_cells, y_cells)
    moves += [(pot.at[z_cells - 1], z_up.at[rows]), (pot.at[0], z_down.at[rows])]
    planes = [
        pltpu.make_async_copy(a, b, plane_sem.at[i]) for i, (a, b) in enumerate(moves)
    ]
    for copy in fields + edges + planes:
        copy.start()
    picked[...] = jnp.zeros_like(picked)
    lane = lax.broadcasted_iota(jnp.int32, (1, lanes), 1)

    for copy in lists:
        copy.wait()

    def listed(r, found):
        z = rec[0, 0, r] - z_first
        y = rec[1, 0, r] - y_first
        near[found] = r
        inside = (z >= 0) & (z < z_cells) & (y >= 0) & (y < y_cells)
        return found + inside.astype(jnp.int32)

    found = lax.fori_loop(0, count, listed, 0, unroll=8)
    for copy in fields:
        copy.wait()

    def one(n, carry):
        r = near[n]
        z = jnp.clip(rec[0, 0, r] - z_first, 0, z_cells - 1)
        y = jnp.clip(rec[1, 0, r] - y_first, 0, y_cells - 1)
        row = field[z, pl.ds(y, 1), :] - obs[0, r]
        picked[pl.ds(r, 1), :] = jnp.where(lane == rec[2, 0, r], row, 0.0)
        return carry

    lax.fori_loop(0, found, one, 0)
    column = jnp.sum(picked[...], axis=1, keepdims=True)
    eye = lax.broadcasted_iota(jnp.int32, (count, lanes), 0) == lax.broadcasted_iota(
        jnp.int32, (count, lanes), 1
    )
    values = jnp.sum(jnp.where(eye, column, 0.0), axis=0, keepdims=True)

    for copy in edges:
        copy.wait()
    for k in range(z_cells):
        y_down[k, 0:3, :] = rims[0, k, 0:3, :]
        y_down[k, 3:6, :] = rims[2, k, 0:3, :]
        y_down[k, 6:7, :] = rims[4, k, 0:1, :]
        y_down[k, 7:8, :] = values
        y_up[k, 0:3, :] = rims[1, k, 5:8, :]
        y_up[k, 3:6, :] = rims[3, k, 5:8, :]
        y_up[k, 6:7, :] = rims[5, k, 7:8, :]
        y_up[k, 7:8, :] = values
    for k in range(W):
        top = z_cells - W + k
        down_down[k] = y_down[k]
        down_up[k] = y_up[k]
        up_down[k] = y_down[top]
        up_up[k] = y_up[top]
    z_down[last : last + 8, :] = jnp.broadcast_to(values, (8, lanes))
    z_up[last : last + 8, :] = jnp.broadcast_to(values, (8, lanes))
    for copy in planes:
        copy.wait()


def rim_rows(sub, low, high, first, depth):
    below = jnp.where(sub >= 8 - depth, pltpu.roll(low, (8 - depth - first) % 8, 0), 0.0)
    above = jnp.where(sub < depth, pltpu.roll(high, (8 - first) % 8, 0) if first else high, 0.0)
    return below, above


def piece(ref, k, j, chunks):
    return ref[k, pl.ds(8 * j, 8), :] if 0 <= j < chunks + 2 else jnp.zeros((8, ref.shape[2]), F32)


def weight_kernel(
    cond, c_lo, c_hi, d_lo, d_hi, y_lo, y_hi, lo_lo, lo_hi, hi_lo, hi_hi,
    we, tx, ty, tz, ce,
):
    z_cells, y_cells, lanes = cond.shape
    chunks = y_cells // 8
    planes = z_cells + 2 * W
    z_first = lax.axis_index("gz") * z_cells
    y_first = lax.axis_index("gy") * y_cells
    z_total = lax.axis_size("gz") * z_cells
    y_total = lax.axis_size("gy") * y_cells
    sub = lax.broadcasted_iota(jnp.int32, (8, lanes), 0)
    lane = lax.broadcasted_iota(jnp.int32, (8, lanes), 1)
    right = lanes - 1
    body = pl.ds(8, y_cells)
    end = pl.ds(y_cells + 8, 8)
    for k in range(z_cells):
        ce[W + k, body, :] = cond[k]
    for k in range(planes):
        if k < W:
            low, high = lo_lo[k], lo_hi[k]
        elif k < W + z_cells:
            low, high = y_lo[k - W], y_hi[k - W]
        else:
            low, high = hi_lo[k - W - z_cells], hi_hi[k - W - z_cells]
        ce[k, 0:8, :], ce[k, end, :] = rim_rows(sub, low, high, 0, 3)
    direct = lax.axis_index("pat") == 1

    @pl.when(direct)
    def _():
        for k in range(W):
            ce[k, body, :] = c_lo[k]
            ce[W + z_cells + k, body, :] = c_hi[k]

    @pl.when(jnp.logical_not(direct))
    def _():
        for k in range(W):
            ce[k, body, :] = d_lo[k]
            ce[W + z_cells + k, body, :] = d_hi[k]

    for j in range(chunks + 2):
        at = pl.ds(8 * j, 8)
        tz[0, at, :] = ce[0, at, :] + ce[1, at, :]

    def plane(k, carry):
        z = z_first + k - W
        z_inside = (z >= 0) & (z < z_total)
        c_up = pltpu.roll(piece(ce, k, 0, chunks), 7, 0)
        face_before = jnp.zeros((8, lanes), F32)
        for j in range(chunks + 2):
            at = pl.ds(8 * j, 8)
            c = piece(ce, k, j, chunks)
            c_next = pltpu.roll(piece(ce, k, j + 1, chunks), 7, 0)
            face_y = c + jnp.where(sub == 7, c_next, c_up)
            face_y_down = pltpu.roll(face_y, 1, 0)
            face_x = c + pltpu.roll(c, right, 1)
            face_z = c + ce[k + 1, at, :]
            total = face_y + jnp.where(sub == 0, face_before, face_y_down)
            total += jnp.where(lane == right, c, face_x)
            total += jnp.where(lane == 0, c, pltpu.roll(face_x, 1, 1))
            total += face_z + tz[k - 1, at, :]
            y = sub + (y_first + 8 * j - 8)
            known = z_inside & (y >= 0) & (y < y_total)
            if j == 0:
                known = known & (sub >= 5)
            if j == chunks + 1:
                known = known & (sub < 3)
            we[k, at, :] = jnp.where(known, 0.8 / jnp.where(known, total, 1.0), 0.0)
            tx[k, at, :] = jnp.where(lane == right, 0.0, face_x)
            ty[k, at, :] = face_y
            tz[k, at, :] = face_z
            c_up, face_before = c_next, face_y_down
        return carry

    lax.fori_loop(1, planes - 1, plane, 0)


def sweep_kernel(
    rec_hbm, adj, we, tx, ty, tz, z_lo, z_hi, y_lo, y_hi, lo_lo, lo_hi, hi_lo, hi_hi, own,
    ae, be, vals, rec, near, list_sem,
):
    z_cells, y_cells, lanes = adj.shape
    count = vals.shape[0]
    chunks = y_cells // 8
    planes = z_cells + 2 * W
    z_first = lax.axis_index("gz") * z_cells
    y_first = lax.axis_index("gy") * y_cells
    sub = lax.broadcasted_iota(jnp.int32, (8, lanes), 0)
    lane = lax.broadcasted_iota(jnp.int32, (1, lanes), 1)
    right = lanes - 1
    body = pl.ds(8, y_cells)
    end = pl.ds(y_cells + 8, 8)
    listing = pltpu.make_async_copy(rec_hbm, rec, list_sem)
    listing.start()
    for k in range(planes):
        if k < W:
            low, high = lo_lo[k], lo_hi[k]
            ae[k, body, :] = z_lo[k * y_cells : (k + 1) * y_cells, :]
        elif k < W + z_cells:
            low, high = y_lo[k - W], y_hi[k - W]
            ae[k, body, :] = adj[k - W]
        else:
            n = k - W - z_cells
            low, high = hi_lo[n], hi_hi[n]
            ae[k, body, :] = z_hi[n * y_cells : (n + 1) * y_cells, :]
        ae[k, 0:8, :], ae[k, end, :] = rim_rows(sub, low, high, 3, 3)

    last = (W + 1) * y_cells
    values = own[0, 7:8, :] + z_lo[last : last + 1, :] + z_hi[last : last + 1, :]
    for side in (y_lo, y_hi, lo_lo, lo_hi, hi_lo, hi_hi):
        values += side[0, 7:8, :]
    eye = lax.broadcasted_iota(jnp.int32, (count, lanes), 0) == lax.broadcasted_iota(
        jnp.int32, (count, lanes), 1
    )
    vals[...] = jnp.broadcast_to(
        jnp.sum(jnp.where(eye, values, 0.0), axis=1, keepdims=True), (count, lanes)
    )
    listing.wait()

    def listed(r, found):
        k = rec[0, 0, r] - z_first + W
        j = rec[1, 0, r] - y_first + 8
        near[found] = r
        inside = (k >= 1) & (k < planes - 1) & (j >= 6) & (j < y_cells + 10)
        return found + inside.astype(jnp.int32)

    found = lax.fori_loop(0, count, listed, 0, unroll=8)

    def sweep(source, target, start, stop):
        def plane(k, carry):
            f_up = pltpu.roll(piece(source, k, 0, chunks), 7, 0)
            flux_before = jnp.zeros((8, lanes), F32)
            for j in range(chunks + 2):
                at = pl.ds(8 * j, 8)
                f = piece(source, k, j, chunks)
                f_next = pltpu.roll(piece(source, k, j + 1, chunks), 7, 0)
                face_x, face_y = tx[k, at, :], ty[k, at, :]
                flux_down = pltpu.roll(face_y * f, 1, 0)
                total = face_y * jnp.where(sub == 7, f_next, f_up)
                total += jnp.where(sub == 0, flux_before, flux_down)
                total += face_x * pltpu.roll(f, right, 1) + pltpu.roll(face_x * f, 1, 1)
                total += tz[k, at, :] * source[k + 1, at, :] + tz[k - 1, at, :] * source[k - 1, at, :]
                target[k, at, :] = 0.2 * f + we[k, at, :] * total
                f_up, flux_before = f_next, flux_down
            return carry

        lax.fori_loop(start, stop, plane, 0)

        def one(n, carry):
            r = near[n]
            k = rec[0, 0, r] - z_first + W
            at = pl.ds(jnp.clip(rec[1, 0, r] - y_first + 8, 6, y_cells + 9), 1)

            @pl.when((k >= start) & (k < stop))
            def _():
                kc = jnp.clip(k, start, stop - 1)
                add = 2.0 * we[kc, at, :] * vals[pl.ds(r, 1), :]
                target[kc, at, :] = target[kc, at, :] + jnp.where(lane == rec[2, 0, r], add, 0.0)

            return carry

        lax.fori_loop(0, found, one, 0)

    sweep(ae, be, 1, planes - 1)
    sweep(be, ae, 2, planes - 2)


def gradient_kernel(pot, ae, z_lo, z_hi, y_lo, y_hi, grad, adj_out, ve, out_sem):
    z_cells, y_cells, lanes = pot.shape
    chunks = y_cells // 8
    sub = lax.broadcasted_iota(jnp.int32, (8, lanes), 0)
    lane = lax.broadcasted_iota(jnp.int32, (8, lanes), 1)
    right = lanes - 1
    body = pl.ds(8, y_cells)
    end = pl.ds(y_cells + 8, 8)
    stores = [
        pltpu.make_async_copy(ae.at[W + k, body], adj_out.at[k], out_sem.at[k])
        for k in range(z_cells)
    ]
    for copy in stores:
        copy.start()
    plane_rows = slice(W * y_cells, (W + 1) * y_cells)
    ve[0, body, :] = z_lo[plane_rows, :]
    ve[z_cells + 1, body, :] = z_hi[plane_rows, :]
    for k in range(z_cells):
        ve[1 + k, body, :] = pot[k]
        ve[1 + k, 0:8, :], ve[1 + k, end, :] = rim_rows(sub, y_lo[k], y_hi[k], 6, 1)

    def plane(n, carry):
        k, q = n + W, n + 1

        def up(ref, m, j):
            return pltpu.roll(piece(ref, m, j, chunks), 7, 0)

        a, v = piece(ae, k, 0, chunks), piece(ve, q, 0, chunks)
        a_up, v_up = up(ae, k, 1), up(ve, q, 1)
        term_before = pltpu.roll(
            (v - jnp.where(sub == 7, v_up, v)) * (a - jnp.where(sub == 7, a_up, a)), 1, 0
        )
        for j in range(1, chunks + 1):
            at = pl.ds(8 * j, 8)
            a, v = piece(ae, k, j, chunks), piece(ve, q, j, chunks)
            a_next, v_next = up(ae, k, j + 1), up(ve, q, j + 1)
            term = (v - jnp.where(sub == 7, v_next, v_up)) * (a - jnp.where(sub == 7, a_next, a_up))
            term_down = pltpu.roll(term, 1, 0)
            total = term + jnp.where(sub == 0, term_before, term_down)
            term = (v - jnp.where(lane == right, 0.0, pltpu.roll(v, right, 1))) * (
                a - jnp.where(lane == right, 0.0, pltpu.roll(a, right, 1))
            )
            total += term + jnp.where(lane == 0, v * a, pltpu.roll(term, 1, 1))
            total += (v - ve[q - 1, at, :]) * (a - ae[k - 1, at, :])
            total += (v - ve[q + 1, at, :]) * (a - ae[k + 1, at, :])
            grad[n, pl.ds(8 * (j - 1), 8), :] = -0.5 * total
            term_before, a_up, v_up = term_down, a_next, v_next
        return carry

    lax.fori_loop(0, z_cells, plane, 0)
    for copy in stores:
        copy.wait()


def shifts(devices, step):
    return [(i, i + step) for i in range(devices) if 0 <= i + step < devices]


def both_ways(up, down, axis):
    devices = lax.axis_size(axis)
    return (
        lax.ppermute(up, axis, shifts(devices, 1)), lax.ppermute(down, axis, shifts(devices, -1))
    )


def step(conductivity, receivers, observed, potential, adjoint_prev):
    cond, pot, adj = conductivity, potential[0], adjoint_prev[0]
    z_cells, y_cells, lanes = cond.shape
    count = observed.shape[1]
    shape = jax.ShapeDtypeStruct

    block = shape((z_cells, y_cells, lanes), F32)
    edge = shape((z_cells, 8, lanes), F32)
    side = shape(((W + 1) * y_cells + 8, lanes), F32)
    thick = shape((W, y_cells, lanes), F32)
    corner = shape((W, 8, lanes), F32)
    rec = receivers.transpose(1, 0, 2)
    rec, obs, cond, adj, pot = (
        pltpu.with_memory_space_constraint(x, pltpu.HBM) for x in (rec, observed, cond, adj, pot)
    )
    z_down, z_up, c_down, c_up, y_down, y_up, dd, du, ud, uu = pl.pallas_call(
        pack_kernel,
        out_shape=(side, side, thick, thick, edge, edge) + (corner,) * 4,
        in_specs=[HBM] * 5,
        out_specs=(VMEM,) * 10,
        scratch_shapes=[
            pltpu.VMEM((count, lanes), F32),
            pltpu.VMEM((z_cells, y_cells, lanes), F32),
            pltpu.VMEM((6, z_cells, 8, lanes), F32),
            pltpu.SMEM((3, 1, count), jnp.int32),
            pltpu.SMEM((1, count), F32),
            pltpu.SMEM((count,), jnp.int32),
            pltpu.SemaphoreType.DMA((6,)),
            pltpu.SemaphoreType.DMA((z_cells,)),
            pltpu.SemaphoreType.DMA((4 * W + 2,)),
            pltpu.SemaphoreType.DMA((2,)),
        ],
        compiler_params=pltpu.CompilerParams(vmem_limit_bytes=16 * 1024 * 1024),
        name="pack",
    )(rec, obs, cond, adj, pot)

    deep = lax.axis_size("gz")
    c_lo = lax.ppermute(c_up, ("gz", "pat"), [(2 * i + 1, 2 * i + 3) for i in range(deep - 1)])
    c_hi = lax.ppermute(c_down, ("gz", "pat"), [(2 * i + 3, 2 * i + 1) for i in range(deep - 1)])
    z_lo, z_hi = both_ways(z_up, z_down, "gz")
    y_lo, y_hi = both_ways(y_up, y_down, "gy")
    wide = lax.axis_size("gy")

    def diagonal(x, up_z, up_y):
        pairs = [
            (i * wide + j, (i + up_z) * wide + j + up_y)
            for i in range(deep) if 0 <= i + up_z < deep
            for j in range(wide) if 0 <= j + up_y < wide
        ]
        return lax.ppermute(x, ("gz", "gy"), pairs)

    lo_lo = diagonal(uu, 1, 1)
    lo_hi = diagonal(ud, 1, -1)
    hi_lo = diagonal(du, -1, 1)
    hi_hi = diagonal(dd, -1, -1)
    d_lo = lax.ppermute(c_lo, "pat", [(1, 0)])
    d_hi = lax.ppermute(c_hi, "pat", [(1, 0)])

    full = (z_cells + 2 * W, y_cells + 16, lanes)
    ext = shape(full, F32)
    we, tx, ty, tz = pl.pallas_call(
        weight_kernel,
        out_shape=(ext,) * 4,
        in_specs=[VMEM] * 11,
        out_specs=(VMEM,) * 4,
        scratch_shapes=[pltpu.VMEM(full, F32)],
        compiler_params=pltpu.CompilerParams(vmem_limit_bytes=20 * 1024 * 1024),
        name="weights",
    )(conductivity, c_lo, c_hi, d_lo, d_hi, y_lo, y_hi, lo_lo, lo_hi, hi_lo, hi_hi)
    relaxed = pl.pallas_call(
        sweep_kernel,
        out_shape=ext,
        in_specs=[HBM] + [VMEM] * 14,
        out_specs=VMEM,
        scratch_shapes=[
            pltpu.VMEM(full, F32),
            pltpu.VMEM((count, lanes), F32),
            pltpu.SMEM((3, 1, count), jnp.int32),
            pltpu.SMEM((count,), jnp.int32),
            pltpu.SemaphoreType.DMA,
        ],
        compiler_params=pltpu.CompilerParams(vmem_limit_bytes=20 * 1024 * 1024),
        name="sweeps",
    )(rec, adjoint_prev[0], we, tx, ty, tz, z_lo, z_hi, y_lo, y_hi, lo_lo, lo_hi, hi_lo, hi_hi, y_up)
    part, adjoint = pl.pallas_call(
        gradient_kernel,
        out_shape=(block, block),
        in_specs=[VMEM] * 6,
        out_specs=(VMEM, HBM),
        scratch_shapes=[
            pltpu.VMEM((z_cells + 2, y_cells + 16, lanes), F32),
            pltpu.SemaphoreType.DMA((z_cells,)),
        ],
        compiler_params=pltpu.CompilerParams(vmem_limit_bytes=16 * 1024 * 1024),
        name="gradient",
    )(potential[0], relaxed, z_lo, z_hi, y_lo, y_hi)
    other = lax.ppermute(part, "pat", [(0, 1), (1, 0)])
    return adjoint[None], part + other


def solution(mesh):
    return jax.shard_map(
        step,
        mesh=mesh,
        in_specs=(
            P(("survey", "gz"), "gy", None),
            P(("survey", "pat"), None, None),
            P(("survey", "pat"), None),
            P("pat", ("survey", "gz"), "gy", None),
            P("pat", ("survey", "gz"), "gy", None),
        ),
        out_specs=(P("pat", ("survey", "gz"), "gy", None), P(("survey", "gz"), "gy", None)),
        check_vma=False,
    )
```

time: 118 us -> 110 us (0.932)
  blocking collectives: 39 us -> 0 us
  starting transfers between devices: 37.3 us -> 67.4 us
  other arithmetic: 27.6 us -> 1.18 us
  waiting for transfers between devices: 7.83 us -> 25.7 us
  Pallas kernels: 0 us -> 13.4 us
  local copies, waits for them, and re-layouts: 4.08 us -> 0.02 us
    all_to_all x1 -> x0, blocking collectives: 39 us -> none  [from_everyone(): lax.all_to_all(jnp.broadcast_to(x[None], (devices, *x.shape)), axis, 0, 0...]
    ppermute x12 -> x13, starting transfers between devices: 37.3 us -> 67.4 us  [the longest x1 32.8 us: step(): d_lo = lax.ppermute(c_lo, 'pat', [(1, 0)])]
    ppermute x12 -> x13, waiting for transfers between devices: 7.83 us -> 25.7 us  [the longest x4 16.7 us: diagonal(): return lax.ppermute(x, ('gz', 'gy'), pairs)]
    pallas_call x0 -> x4, Pallas kernels: none -> 13.4 us  [the longest x1 4.92 us: step(): pl.pallas_call(sweep_kernel, out_shape=ext, in_specs=[HBM] + [VMEM] * 14,...]
    scatter-add x1 -> x0, other arithmetic: 9.7 us -> none  [receiver_source(): jnp.zeros_like(field).at[pattern_ids, z_local, y_local, x_local].add(values)]
    add x2 -> x1, other arithmetic: 8.08 us -> 1.18 us  [step(): return (adjoint[None], part + other)]
    broadcast_in_dim x1 -> x0, other arithmetic: 3.47 us -> none  [from_everyone(): jnp.broadcast_to(x[None], (devices, *x.shape))]
    concatenate x7 -> x0, other arithmetic: 2.97 us -> none  [the longest x3 2.84 us: extended_2(): jnp.concatenate([jnp.pad(low, around), x, jnp.pad(high, around)], axis=dim)]
  transfers between devices with their start and end apart: 12 -> 13, of which waited for: 3 -> 6; matrix products, arithmetic and copies ran while one was open for 11% -> 0% of each run, Pallas kernels for 0% -> 3%
where the time goes in v1:
time: 110 us; the launch traced here: 108 us
  starting transfers between devices  67.4 us (61%)
  waiting for transfers between devices  25.7 us (23%)
  Pallas kernels  13.4 us (12%)
  other arithmetic  1.18 us (1%)
    ppermute x1, starting transfers between devices, step(): d_lo = lax.ppermute(c_lo, 'pat', [(1, 0)])  32.8 us
    ppermute x4, waiting for transfers between devices, diagonal(): return lax.ppermute(x, ('gz', 'gy'), pairs)  16.7 us
    ppermute x1, starting transfers between devices, step(): other = lax.ppermute(part, 'pat', [(0, 1), (1, 0)])  12.3 us
    ppermute x2, starting transfers between devices, both_ways(): lax.ppermute(up, axis, shifts(devices, 1))  7.65 us
    ppermute x1, starting transfers between devices, step(): lax.ppermute(c_up, ('gz', 'pat'), [(2 * i + 1, 2 * i + 3) for i in range(...  5.4 us
    pallas_call x1, Pallas kernels, step(): pl.pallas_call(sweep_kernel, out_shape=ext, in_specs=[HBM] + [VMEM] * 14,...  4.92 us
    ppermute x4, starting transfers between devices, diagonal(): return lax.ppermute(x, ('gz', 'gy'), pairs)  3.93 us
    ppermute x2, waiting for transfers between devices, both_ways(): lax.ppermute(down, axis, shifts(devices, -1))  3.73 us
  transfers between devices with their start and end apart: 13, of which 6 were waited for; matrix products, arithmetic and copies ran while one was open for 0% of the time, Pallas kernels for 3%

profile of v1, /device:TPU:33, one launch (start us, length us, event | category | flops | bytes accessed | tf_op | source)
XLA Modules:
  0.0 108.5 jit_solution(14910364472659488559)
XLA Ops:
  0.6 2.8 %pack.1 = (f32[520,512]{1,0:T(8,128)S(1)}, f32[520,512]{1,0:T(8,128)S(1)}, f32[3,128,512]{2,1,0:T(8,128)S(1)}, f32[3,128,512]{2,1,0:T(8,128)S(1)}, f32[4,8,512]{...) custom-call(s32[3,1,64]{2,1,0:T(1,128)} %bitcast.8, ...), custom_call_target="tpu_custom_call" | custom-call | tf_op jit(solution)/shard_map/pack/pallas_call | solution.py:365
  3.5 0.0 copy-start.2
  3.5 5.4 %collective-permute-start = (f32[3,128,512]{2,1,0:T(8,128)S(1)}, f32[3,128,512]{2,1,0:T(8,128)S(1)}, u32[]{:S(2)}, u32[]{:S(2)}) collective-permute-start(f32[3,128,512]{2,1,0:T(8,128)S(1)} %get-tuple-element.18), channel_id=1, source_target_pairs={{1,9},{9,17},{17,25},{25,33},{33,41},{41,49},{49,57},{57,65},{65,7... | collective-permute-start | bytes 2359304 | tf_op jit(solution)/shard_map/ppermute | solution.py:387
  8.9 1.3 %collective-permute-start.1 = (f32[3,128,512]{2,1,0:T(8,128)S(1)}, f32[3,128,512]{2,1,0:T(8,128)S(1)}, u32[]{:S(2)}, u32[]{:S(2)}) collective-permute-start(f32[3,128,512]{2,1,0:T(8,128)S(1)} %get-tuple-element.19), channel_id=1, source_target_pairs={{9,1},{17,9},{25,17},{33,25},{41,33},{49,41},{57,49},{65,57},{73,6... | collective-permute-start | bytes 2359304 | tf_op jit(solution)/shard_map/ppermute | solution.py:388
  10.2 5.1 %collective-permute-start.10 = (f32[520,512]{1,0:T(8,128)S(1)}, f32[520,512]{1,0:T(8,128)S(1)}, u32[]{:S(2)}, u32[]{:S(2)}) collective-permute-start(f32[520,512]{1,0:T(8,128)S(1)} %get-tuple-element.30), channel_id=1, source_target_pairs={{0,8},{8,16},{16,24},{24,32},{32,40},{40,48},{48,56},{56,64},{64,7... | collective-permute-start | bytes 3194888 | tf_op jit(solution)/shard_map/ppermute | solution.py:346
  15.3 1.3 %collective-permute-start.11 = (f32[520,512]{1,0:T(8,128)S(1)}, f32[520,512]{1,0:T(8,128)S(1)}, u32[]{:S(2)}, u32[]{:S(2)}) collective-permute-start(f32[520,512]{1,0:T(8,128)S(1)} %get-tuple-element.31), channel_id=1, source_target_pairs={{8,0},{16,8},{24,16},{32,24},{40,32},{48,40},{56,48},{64,56},{72,6... | collective-permute-start | bytes 3194888 | tf_op jit(solution)/shard_map/ppermute | solution.py:346
  16.7 1.7 %collective-permute-done.c_lo = f32[3,128,512]{2,1,0:T(8,128)S(1)} collective-permute-done((f32[3,128,512]{2,1,0:T(8,128)S(1)}, f32[3,128,512]{2,1,0:T(8,128)S(1)}, u32[]{:S(2)}, u32[]{:S(2)}) %collective-permute-start) | collective-permute-done | bytes 786464 | tf_op jit(solution)/shard_map/ppermute | solution.py:387
  18.4 32.8 %collective-permute-start.2 = (f32[3,128,512]{2,1,0:T(8,128)S(1)}, f32[3,128,512]{2,1,0:T(8,128)S(1)}, u32[]{:S(2)}, u32[]{:S(2)}) collective-permute-start(f32[3,128,512]{2,1,0:T(8,128)S(1)} %collective-permute-done.c_lo), channel_id=1, source_target_pairs={{1,0},{3,2},{5,4},{7,6},{9,8},{11,10},{13,12},{15,14},{17,16},{19,... | collective-permute-start | bytes 2359304 | tf_op jit(solution)/shard_map/ppermute | solution.py:405
  51.2 0.0 collective-permute-done.1.c_hi
  51.2 1.4 %collective-permute-start.3 = (f32[3,128,512]{2,1,0:T(8,128)S(1)}, f32[3,128,512]{2,1,0:T(8,128)S(1)}, u32[]{:S(2)}, u32[]{:S(2)}) collective-permute-start(f32[3,128,512]{2,1,0:T(8,128)S(1)} %collective-permute-done.1.c_hi), channel_id=1, source_target_pairs={{1,0},{3,2},{5,4},{7,6},{9,8},{11,10},{13,12},{15,14},{17,16},{19,... | collective-permute-start | bytes 2359304 | tf_op jit(solution)/shard_map/ppermute | solution.py:406
  52.5 1.3 %collective-permute-start.6 = (f32[3,8,512]{2,1,0:T(8,128)S(1)}, f32[3,8,512]{2,1,0:T(8,128)S(1)}, u32[]{:S(2)}, u32[]{:S(2)}) collective-permute-start(f32[3,8,512]{2,1,0:T(8,128)S(1)} %get-tuple-element.22), channel_id=1, source_target_pairs={{0,10},{2,12},{4,14},{8,18},{10,20},{12,22},{16,26},{18,28},{20,30... | collective-permute-start | bytes 147464 | tf_op jit(solution)/shard_map/ppermute | solution.py:399
  53.9 1.5 %collective-permute-done.6.lo_lo = f32[3,8,512]{2,1,0:T(8,128)S(1)} collective-permute-done((f32[3,8,512]{2,1,0:T(8,128)S(1)}, f32[3,8,512]{2,1,0:T(8,128)S(1)}, u32[]{:S(2)}, u32[]{:S(2)}) %collective-permute-start.6) | collective-permute-done | bytes 49184 | tf_op jit(solution)/shard_map/ppermute | solution.py:399
  55.4 0.7 collective-permute-start.7
  56.1 0.0 collective-permute-done.7.lo_hi
  56.1 0.7 collective-permute-start.8
  56.7 0.0 collective-permute-done.8.hi_lo
  56.7 1.3 %collective-permute-start.9 = (f32[3,8,512]{2,1,0:T(8,128)S(1)}, f32[3,8,512]{2,1,0:T(8,128)S(1)}, u32[]{:S(2)}, u32[]{:S(2)}) collective-permute-start(f32[3,8,512]{2,1,0:T(8,128)S(1)} %get-tuple-element.25), channel_id=1, source_target_pairs={{10,0},{12,2},{14,4},{18,8},{20,10},{22,12},{26,16},{28,18},{30,20... | collective-permute-start | bytes 147464 | tf_op jit(solution)/shard_map/ppermute | solution.py:399
  58.1 15.1 %collective-permute-done.9.hi_hi = f32[3,8,512]{2,1,0:T(8,128)S(1)} collective-permute-done((f32[3,8,512]{2,1,0:T(8,128)S(1)}, f32[3,8,512]{2,1,0:T(8,128)S(1)}, u32[]{:S(2)}, u32[]{:S(2)}) %collective-permute-start.9) | collective-permute-done | bytes 49184 | tf_op jit(solution)/shard_map/ppermute | solution.py:399
  73.2 1.3 %collective-permute-start.5 = (f32[4,8,512]{2,1,0:T(8,128)S(1)}, f32[4,8,512]{2,1,0:T(8,128)S(1)}, u32[]{:S(2)}, u32[]{:S(2)}) collective-permute-start(f32[4,8,512]{2,1,0:T(8,128)S(1)} %get-tuple-element.21), channel_id=1, source_target_pairs={{2,0},{4,2},{6,4},{3,1},{5,3},{7,5},{10,8},{12,10},{14,12},{11,9},... | collective-permute-start | bytes 196616 | tf_op jit(solution)/shard_map/ppermute | solution.py:346
  74.5 3.7 %collective-permute-done.5.y_hi = f32[4,8,512]{2,1,0:T(8,128)S(1)} collective-permute-done((f32[4,8,512]{2,1,0:T(8,128)S(1)}, f32[4,8,512]{2,1,0:T(8,128)S(1)}, u32[]{:S(2)}, u32[]{:S(2)}) %collective-permute-start.5) | collective-permute-done | bytes 65568 | tf_op jit(solution)/shard_map/ppermute | solution.py:346
  78.2 2.5 %collective-permute-start.4 = (f32[4,8,512]{2,1,0:T(8,128)S(1)}, f32[4,8,512]{2,1,0:T(8,128)S(1)}, u32[]{:S(2)}, u32[]{:S(2)}) collective-permute-start(f32[4,8,512]{2,1,0:T(8,128)S(1)} %get-tuple-element.20.own), channel_id=1, source_target_pairs={{0,2},{2,4},{4,6},{1,3},{3,5},{5,7},{8,10},{10,12},{12,14},{9,11},... | collective-permute-start | bytes 196616 | tf_op jit(solution)/shard_map/ppermute | solution.py:346
  80.7 1.3 %collective-permute-done.4.y_lo = f32[4,8,512]{2,1,0:T(8,128)S(1)} collective-permute-done((f32[4,8,512]{2,1,0:T(8,128)S(1)}, f32[4,8,512]{2,1,0:T(8,128)S(1)}, u32[]{:S(2)}, u32[]{:S(2)}) %collective-permute-start.4) | collective-permute-done | bytes 65568 | tf_op jit(solution)/shard_map/ppermute | solution.py:346
  82.1 0.0 collective-permute-done.2.d_lo
  82.1 0.0 collective-permute-done.3.d_hi
  82.1 2.8 %weights.1 = (f32[10,144,512]{2,1,0:T(8,128)S(1)}, f32[10,144,512]{2,1,0:T(8,128)S(1)}, f32[10,144,512]{2,1,0:T(8,128)S(1)}, f32[10,144,512]{2,1,0:T(8,128)S(1)}) custom-call(f32[4,128,512]{2,1,0:T(8,128)S(1)} %copy-done, f32[3,128,512]{2,1,0:T(8,128)S(1)} %collective-permute-done.c_lo, f32[3,128,512]{2,1,0:T(8,128)S(1)} %collective-permute-done.1.c_hi, ...), custom_call_target="tpu_custom_call" | custom-call | tf_op jit(solution)/shard_map/weights/pallas_call | solution.py:410
  84.9 0.0 collective-permute-done.10.z_lo
  84.9 0.0 copy-start.1
  84.9 4.9 %sweeps.1.ae = f32[10,144,512]{2,1,0:T(8,128)S(1)} custom-call(s32[3,1,64]{2,1,0:T(1,128)} %bitcast.9, f32[4,128,512]{2,1,0:T(8,128)S(1)} %bitcast.7, f32[10,144,512]{2,1,0:T(8,128)S(1)} %get-tuple-element.26.we, f32[10,144,512]{2,1,0:T(8,128)S(1)} %get-tuple-element.27.tx, f32[10,144,512]{2,1,0:T(8,128)S(1)} %get-tuple-element.28.ty, ...), custom_call_target="tpu_custom_call" | custom-call | tf_op jit(solution)/shard_map/sweeps/pallas_call | solution.py:419
  89.9 2.8 %gradient.1 = (f32[4,128,512]{2,1,0:T(8,128)S(1)}, f32[4,128,512]{2,1,0:T(8,128)}) custom-call(f32[4,128,512]{2,1,0:T(8,128)S(1)} %bitcast.5, f32[10,144,512]{2,1,0:T(8,128)S(1)} %sweeps.1.ae, f32[520,512]{1,0:T(8,128)S(1)} %collective-permute-done.10.z_lo, f32[520,512]{1,0:T(8,128)S(1)} %collective-permute-done.11.z_hi, ...), custom_call_target="tpu_custom_call" | custom-call | tf_op jit(solution)/shard_map/gradient/pallas_call | solution.py:434
  92.7 12.3 %collective-permute-start.12 = (f32[4,128,512]{2,1,0:T(8,128)S(1)}, f32[4,128,512]{2,1,0:T(8,128)S(1)}, u32[]{:S(2)}, u32[]{:S(2)}) collective-permute-start(f32[4,128,512]{2,1,0:T(8,128)S(1)} %get-tuple-element.33), channel_id=1, source_target_pairs={{0,1},{1,0},{2,3},{3,2},{4,5},{5,4},{6,7},{7,6},{8,9},{9,8},{10,11... | collective-permute-start | bytes 3145736 | tf_op jit(solution)/shard_map/ppermute | solution.py:446
  105.0 2.3 %collective-permute-done.12 = f32[4,128,512]{2,1,0:T(8,128)S(1)} collective-permute-done((f32[4,128,512]{2,1,0:T(8,128)S(1)}, f32[4,128,512]{2,1,0:T(8,128)S(1)}, u32[]{:S(2)}, u32[]{:S(2)}) %collective-permute-start.12) | collective-permute-done | bytes 1048608 | tf_op jit(solution)/shard_map/ppermute | solution.py:446
  107.3 1.2 %add.3 = f32[4,128,512]{2,1,0:T(8,128)} add(f32[4,128,512]{2,1,0:T(8,128)S(1)} %get-tuple-element.33, f32[4,128,512]{2,1,0:T(8,128)S(1)} %collective-permute-done.12) | non-fusion elementwise | flops 262144 | bytes 3145728 | tf_op jit(solution)/shard_map/add | solution.py:447
  (5 shorter events, 0.0 us)
Async XLA Ops:
  0.6 81.4 %copy-start = (f32[4,128,512]{2,1,0:T(8,128)S(1)}, f32[4,128,512]{2,1,0:T(8,128)}, u32[]{:S(2)}) copy-start(f32[4,128,512]{2,1,0:T(8,128)} %cond.3) | copy-start | bytes 3145732
  3.5 81.4 %copy-start.2 = (f32[1,4,128,512]{3,2,1,0:T(8,128)S(1)}, f32[1,4,128,512]{3,2,1,0:T(8,128)}, u32[]{:S(2)}) copy-start(f32[1,4,128,512]{3,2,1,0:T(8,128)} %param.9) | copy-start | bytes 3145732
  3.5 14.9 %collective-permute-start = (f32[3,128,512]{2,1,0:T(8,128)S(1)}, f32[3,128,512]{2,1,0:T(8,128)S(1)}, u32[]{:S(2)}, u32[]{:S(2)}) collective-permute-start(f32[3,128,512]{2,1,0:T(8,128)S(1)} %get-tuple-element.18), channel_id=1, source_target_pairs={{1,9},{9,17},{17,25},{25,33},{33,41},{41,49},{49,57},{57,65},{65,7... | collective-permute-start | bytes 2359304 | tf_op jit(solution)/shard_map/ppermute | solution.py:387
  8.9 42.3 %collective-permute-start.1 = (f32[3,128,512]{2,1,0:T(8,128)S(1)}, f32[3,128,512]{2,1,0:T(8,128)S(1)}, u32[]{:S(2)}, u32[]{:S(2)}) collective-permute-start(f32[3,128,512]{2,1,0:T(8,128)S(1)} %get-tuple-element.19), channel_id=1, source_target_pairs={{9,1},{17,9},{25,17},{33,25},{41,33},{49,41},{57,49},{65,57},{73,6... | collective-permute-start | bytes 2359304 | tf_op jit(solution)/shard_map/ppermute | solution.py:388
  10.2 74.7 %collective-permute-start.10 = (f32[520,512]{1,0:T(8,128)S(1)}, f32[520,512]{1,0:T(8,128)S(1)}, u32[]{:S(2)}, u32[]{:S(2)}) collective-permute-start(f32[520,512]{1,0:T(8,128)S(1)} %get-tuple-element.30), channel_id=1, source_target_pairs={{0,8},{8,16},{16,24},{24,32},{32,40},{40,48},{48,56},{56,64},{64,7... | collective-permute-start | bytes 3194888 | tf_op jit(solution)/shard_map/ppermute | solution.py:346
  15.3 69.6 %collective-permute-start.11 = (f32[520,512]{1,0:T(8,128)S(1)}, f32[520,512]{1,0:T(8,128)S(1)}, u32[]{:S(2)}, u32[]{:S(2)}) collective-permute-start(f32[520,512]{1,0:T(8,128)S(1)} %get-tuple-element.31), channel_id=1, source_target_pairs={{8,0},{16,8},{24,16},{32,24},{40,32},{48,40},{56,48},{64,56},{72,6... | collective-permute-start | bytes 3194888 | tf_op jit(solution)/shard_map/ppermute | solution.py:346
  18.4 63.7 %collective-permute-start.2 = (f32[3,128,512]{2,1,0:T(8,128)S(1)}, f32[3,128,512]{2,1,0:T(8,128)S(1)}, u32[]{:S(2)}, u32[]{:S(2)}) collective-permute-start(f32[3,128,512]{2,1,0:T(8,128)S(1)} %collective-permute-done.c_lo), channel_id=1, source_target_pairs={{1,0},{3,2},{5,4},{7,6},{9,8},{11,10},{13,12},{15,14},{17,16},{19,... | collective-permute-start | bytes 2359304 | tf_op jit(solution)/shard_map/ppermute | solution.py:405
  51.2 30.9 %collective-permute-start.3 = (f32[3,128,512]{2,1,0:T(8,128)S(1)}, f32[3,128,512]{2,1,0:T(8,128)S(1)}, u32[]{:S(2)}, u32[]{:S(2)}) collective-permute-start(f32[3,128,512]{2,1,0:T(8,128)S(1)} %collective-permute-done.1.c_hi), channel_id=1, source_target_pairs={{1,0},{3,2},{5,4},{7,6},{9,8},{11,10},{13,12},{15,14},{17,16},{19,... | collective-permute-start | bytes 2359304 | tf_op jit(solution)/shard_map/ppermute | solution.py:406
  52.5 2.9 %collective-permute-start.6 = (f32[3,8,512]{2,1,0:T(8,128)S(1)}, f32[3,8,512]{2,1,0:T(8,128)S(1)}, u32[]{:S(2)}, u32[]{:S(2)}) collective-permute-start(f32[3,8,512]{2,1,0:T(8,128)S(1)} %get-tuple-element.22), channel_id=1, source_target_pairs={{0,10},{2,12},{4,14},{8,18},{10,20},{12,22},{16,26},{18,28},{20,30... | collective-permute-start | bytes 147464 | tf_op jit(solution)/shard_map/ppermute | solution.py:399
  55.4 0.7 collective-permute-start.7
  56.1 0.7 collective-permute-start.8
  56.7 16.4 %collective-permute-start.9 = (f32[3,8,512]{2,1,0:T(8,128)S(1)}, f32[3,8,512]{2,1,0:T(8,128)S(1)}, u32[]{:S(2)}, u32[]{:S(2)}) collective-permute-start(f32[3,8,512]{2,1,0:T(8,128)S(1)} %get-tuple-element.25), channel_id=1, source_target_pairs={{10,0},{12,2},{14,4},{18,8},{20,10},{22,12},{26,16},{28,18},{30,20... | collective-permute-start | bytes 147464 | tf_op jit(solution)/shard_map/ppermute | solution.py:399
  73.2 5.0 %collective-permute-start.5 = (f32[4,8,512]{2,1,0:T(8,128)S(1)}, f32[4,8,512]{2,1,0:T(8,128)S(1)}, u32[]{:S(2)}, u32[]{:S(2)}) collective-permute-start(f32[4,8,512]{2,1,0:T(8,128)S(1)} %get-tuple-element.21), channel_id=1, source_target_pairs={{2,0},{4,2},{6,4},{3,1},{5,3},{7,5},{10,8},{12,10},{14,12},{11,9},... | collective-permute-start | bytes 196616 | tf_op jit(solution)/shard_map/ppermute | solution.py:346
  78.2 3.9 %collective-permute-start.4 = (f32[4,8,512]{2,1,0:T(8,128)S(1)}, f32[4,8,512]{2,1,0:T(8,128)S(1)}, u32[]{:S(2)}, u32[]{:S(2)}) collective-permute-start(f32[4,8,512]{2,1,0:T(8,128)S(1)} %get-tuple-element.20.own), channel_id=1, source_target_pairs={{0,2},{2,4},{4,6},{1,3},{3,5},{5,7},{8,10},{10,12},{12,14},{9,11},... | collective-permute-start | bytes 196616 | tf_op jit(solution)/shard_map/ppermute | solution.py:346
  84.9 4.9 %copy-start.1 = (f32[1,4,128,512]{3,2,1,0:T(8,128)S(1)}, f32[1,4,128,512]{3,2,1,0:T(8,128)}, u32[]{:S(2)}) copy-start(f32[1,4,128,512]{3,2,1,0:T(8,128)} %param.8) | copy-start | bytes 3145732
  92.7 14.6 %collective-permute-start.12 = (f32[4,128,512]{2,1,0:T(8,128)S(1)}, f32[4,128,512]{2,1,0:T(8,128)S(1)}, u32[]{:S(2)}, u32[]{:S(2)}) collective-permute-start(f32[4,128,512]{2,1,0:T(8,128)S(1)} %get-tuple-element.33), channel_id=1, source_target_pairs={{0,1},{1,0},{2,3},{3,2},{4,5},{5,4},{6,7},{7,6},{8,9},{9,8},{10,11... | collective-permute-start | bytes 3145736 | tf_op jit(solution)/shard_map/ppermute | solution.py:446
